TPU v7x, 32 devices: a whole 2x2x4 slice. The times are simulated.
32 devices in a mesh: grp: 1, dev: 32 (over z, y, x, core).
Axes of the slice: x: 2, y: 2, z: 4, core: 2. Of those that a mesh axis runs over, the one named last changes fastest.
Arguments:
- points: float32 [32768, 768], P(('grp', 'dev')), may hold values from -12 to 12
- assignment: int32 [32768], P(('grp', 'dev')), may hold values from 0 to 8191, as said below
Outputs:
- centroids: float32 [8192, 768], P('dev')
- spread: float32 [8192], P('dev')
Inputs may be any that keep to these rules, and one draw needn't show every extreme that they name: `assignment`: the owner of cluster c is c // 256. Among the 1024 points of one device (aligned blocks of 1024), at most 64 belong to clusters of one owner; some owner receives exactly 64 from every device's block.
All inputs are finite; a program needn't handle non-finite values.
Results may differ from a plain program's by a relative error of at most 0.000071.
Values sent between devices are 32-bit elements; how exact they have to be, the bound alone decides.
A program may use at most 64 MiB of HBM per device.

v0:
```python
import functools

import jax
import jax.numpy as jnp
from jax import lax
from jax.experimental import pallas as pl
from jax.experimental.pallas import tpu as pltpu
from jax.sharding import PartitionSpec as P

CL_OWN = 256
LANES = 128
MESH = pl.DeviceIdType.MESH


def finish(sums, counts, squares):
    denom = jnp.maximum(counts, 1.0)
    centre = sums / denom[:, None]
    spread = (squares - jnp.sum(sums * sums, axis=1) / denom) / (denom * sums.shape[1])
    return (centre, spread)


def pieces(value, count):
    out = []
    for _ in range(count):
        part = value.astype(jnp.bfloat16)
        out.append(part)
        value = value - part.astype(jnp.float32)
    return out


def kernel(
    inner, outer, cap, chunk,
    points_ref, route_ref, sums_ref, aux_ref,
    high, low, facts, hit, hold, cout, xin, yin, mout, mgot, zout, zin, zaux, zin_aux,
    msend, mrecv, csend, crecv, xsend, xrecv, ysend, yrecv, zsend, zrecv, asend, arecv,
):
    me = lax.axis_index("dev")
    plane = me // inner
    seat = lax.rem(me, inner)
    rows, width = points_ref.shape
    chunks = width // chunk
    rep = LANES // cap
    last = outer - 1
    rights, lefts = last - plane, plane

    def target_plane(j):
        if j == last:
            return plane
        right_first = jnp.where(j < rights, last - j, j - rights)
        left_first = jnp.where(j < lefts, j, last - j + lefts)
        return jnp.where(rights > lefts, right_first, left_first)

    def fed(j):
        k = target_plane(j)
        return jnp.where(k > plane, plane > 0, plane < last)

    def across(d):
        other = 0
        for bit in range(3):
            own = lax.rem(seat // 2**bit, 2)
            other = other + (1 - own if d // 2**bit % 2 else own) * 2**bit
        return other

    barrier = pltpu.get_barrier_semaphore()
    for d in range(1, inner):
        peer = plane * inner + across(d)
        pl.semaphore_signal(barrier, inc=1, device_id={"dev": peer}, device_id_type=MESH)
    for d in range(1, outer):
        peer = lax.rem(plane + d, outer) * inner + seat
        pl.semaphore_signal(barrier, inc=1, device_id={"dev": peer}, device_id_type=MESH)
    def plane_copy(src, dst, ssem, rsem, d):
        return pltpu.make_async_remote_copy(
            src_ref=src,
            dst_ref=dst,
            send_sem=ssem,
            recv_sem=rsem,
            device_id={"dev": plane * inner + across(d)},
            device_id_type=MESH,
        )

    core = lax.rem(seat, 2)
    x = lax.rem(seat // 2, 2)
    y = seat // 4

    def core_copy(t):
        j, c = t // chunks, t % chunks
        return plane_copy(
            cout.at[j, c], hold.at[j, c, :, core], csend.at[j, c], crecv.at[j, c], 1
        )

    def core_arrival(t):
        j, c = t // chunks, t % chunks
        return plane_copy(
            cout.at[j, c], hold.at[j, c, :, 1 - core], csend.at[j, c], crecv.at[j, c], 1
        )

    def x_copy(t):
        j, c = t // chunks, t % chunks
        return plane_copy(
            hold.at[j, c, pl.ds((1 - x) * 2, 2)], xin.at[j, c], xsend.at[j, c], xrecv.at[j, c], 2
        )

    def y_copy(t, passed):
        j, c = t // chunks, t % chunks
        source = xin.at[j, c, 1 - y] if passed else hold.at[j, c, x * 2 + 1 - y]
        return plane_copy(
            source, yin.at[j, c, passed], ysend.at[j, c, passed], yrecv.at[j, c, passed], 4
        )

    def meta_copy(d, arriving):
        return plane_copy(
            mout.at[across(d)], mgot.at[across(d) if arriving else seat],
            msend.at[d], mrecv.at[d], d,
        )

    def line_copy(j, c):
        k = target_plane(j)
        step = jnp.where(k > plane, 1, -1)
        place = jnp.where(k == plane - 1, outer, k)
        return pltpu.make_async_remote_copy(
            src_ref=zout.at[j, c],
            dst_ref=zin.at[place, c],
            send_sem=zsend.at[j, c],
            recv_sem=zrecv.at[place, c],
            device_id={"dev": (plane + step) * inner + seat},
            device_id_type=MESH,
        )

    def line_arrival(place, c):
        side = jnp.where(plane > 0, -1, 1)
        return pltpu.make_async_remote_copy(
            src_ref=zout.at[0, c],
            dst_ref=zin.at[place, c],
            send_sem=zsend.at[0, c],
            recv_sem=zrecv.at[place, c],
            device_id={"dev": (plane + side) * inner + seat},
            device_id_type=MESH,
        )

    def aux_copy(j, arriving):
        k = target_plane(j)
        return pltpu.make_async_remote_copy(
            src_ref=zaux.at[j],
            dst_ref=zin_aux.at[k if arriving else plane],
            send_sem=asend.at[j],
            recv_sem=arecv.at[k if arriving else plane],
            device_id={"dev": k * inner + seat},
            device_id_type=MESH,
        )

    steps = outer * chunks
    ahead = 2
    half = inner // 2 * cap

    def picks(j):
        row = lax.broadcasted_iota(jnp.int32, (2 * half, 1), 0)
        slot = target_plane(j) * (2 * half) + row
        slot = slot + jnp.where(row < half, core * half, -core * half)
        return (slot == route_ref[0:1, :]).astype(jnp.bfloat16)

    def gather(t, pick):
        j, c = t // chunks, t % chunks
        columns = slice(c * chunk, (c + 1) * chunk)
        block = jnp.dot(pick, high[:, columns], preferred_element_type=jnp.float32)
        block = block + jnp.dot(pick, low[:, columns], preferred_element_type=jnp.float32)
        hold[j, c, :, core] = block[:half].reshape(inner // 2, cap, chunk)
        cout[j, c] = block[half:].reshape(inner // 2, cap, chunk)
        if t == 0:
            pl.semaphore_wait(barrier, inner + outer - 2)
        core_copy(t).start()

    def launch(t):
        core_arrival(t).wait_recv()
        x_copy(t).start()
        y_copy(t, 0).start()

    def pass_on(t):
        x_copy(t).wait_recv()
        y_copy(t, 1).start()
        if t + ahead < steps:
            launch(t + ahead)

    def tell():
        value = points_ref[...]
        norms = jnp.sum(value * value, axis=1, keepdims=True)
        norms = jnp.broadcast_to(norms, (rows, LANES)).T[0:1, :]
        label = route_ref[1:2, :].astype(jnp.float32).astype(jnp.bfloat16)
        blank = jnp.zeros((4, rows), jnp.bfloat16)
        facts[...] = jnp.concatenate([label] + pieces(norms, 3) + [blank], axis=0)

    def tell_slots(j, pick):
        told = lax.dot_general(
            facts[...], pick, (((1,), (1,)), ((), ())), preferred_element_type=jnp.float32
        )
        for q in range(inner):
            p = q % 2 * 4 + q // 2 % 2 * 2 + (core if q < inner // 2 else 1 - core)
            mine = told[:, q * cap : (q + 1) * cap]
            mout[p, j] = jnp.concatenate([mine] * rep, axis=1)

    lane = lax.broadcasted_iota(jnp.int32, (8, LANES), 1)
    line = lax.broadcasted_iota(jnp.int32, (8, LANES), 0)
    cluster = lax.broadcasted_iota(jnp.int32, (CL_OWN, LANES), 0).astype(jnp.float32) + 1.0

    def matches(j):
        if j == 0:
            for d in range(1, inner):
                meta_copy(d, True).wait_recv()
            mgot[seat] = mout[seat]
        weights = []
        for s in range(inner):
            block = mgot[across(s // 2 * 2) - core + s % 2, j]
            hit[:, s * LANES : (s + 1) * LANES] = (cluster == block[0:1, :]).astype(jnp.bfloat16)
            block = jnp.where(line == 0, 1.0, block)
            weights.append(jnp.where(lane < cap, block, 0.0).astype(jnp.bfloat16))
        aux = lax.dot_general(
            jnp.concatenate(weights, axis=1), hit[...], (((1,), (1,)), ((), ())),
            preferred_element_type=jnp.float32,
        )
        if j < last:
            zaux[j] = aux
            aux_copy(j, False).start()
        else:
            aux_ref[...] = aux

    def reduce(j, c):
        t = j * chunks + c
        y_copy(t, 0).wait_recv()
        y_copy(t, 1).wait_recv()
        stack = []
        for ref in (hold.at[j, c, x * 2 + y], xin.at[j, c, y], yin.at[j, c, 0], yin.at[j, c, 1]):
            for s in range(2):
                stack.extend(pieces(ref[s], rep))
        total = jnp.dot(hit[...], jnp.concatenate(stack, axis=0), preferred_element_type=jnp.float32)
        if j == last:
            sums_ref[:, c * chunk : (c + 1) * chunk] = total
        else:
            zout[j, c] = total

    def forward(j, c):
        @pl.when(fed(j))
        def _():
            k = target_plane(j)
            line_arrival(k, c).wait_recv()
            zout[j, c] += zin[k, c]
            line_copy(j, c).start()

    value = points_ref[...]
    top = value.astype(jnp.bfloat16)
    high[...] = top
    low[...] = (value - top.astype(jnp.float32)).astype(jnp.bfloat16)

    pick = picks(0)
    gather(0, pick)
    tell()
    launch(0)
    for j in range(outer):
        tell_slots(j, picks(j))
    for d in range(1, inner):
        meta_copy(d, False).start()
    for t in range(1, chunks):
        gather(t, pick)
    for t in range(1, ahead):
        if t < chunks:
            launch(t)
    passed = 0
    for j in range(1, outer):
        pick = picks(j)
        for c in range(chunks):
            gather(j * chunks + c, pick)
        if j == 1:
            for t in range(chunks, ahead):
                launch(t)
        if j < outer - 1:
            pass_on(passed)
            passed += 1
    behind = None
    for j in range(outer):
        for c in range(chunks):
            while passed < min(j * chunks + c + 2, steps):
                pass_on(passed)
                passed += 1
            if c == 0:
                matches(j)
            reduce(j, c)
            if j < last:
                @pl.when(jnp.logical_not(fed(j)))
                def _():
                    line_copy(j, c).start()
            if behind is not None:
                forward(*behind)
            behind = (j, c) if j < last else None

    for j in range(last):
        aux_copy(j, True).wait_recv()
        aux_ref[...] += zin_aux[target_plane(j)]
    for c in range(chunks):
        columns = slice(c * chunk, (c + 1) * chunk)

        @pl.when(plane > 0)
        def _():
            line_arrival(plane, c).wait_recv()
            sums_ref[:, columns] += zin[plane, c]

        @pl.when(plane < last)
        def _():
            line_arrival(outer, c).wait_recv()
            sums_ref[:, columns] += zin[outer, c]

    for d in range(1, inner):
        meta_copy(d, False).wait_send()
    for t in range(steps):
        core_copy(t).wait_send()
        x_copy(t).wait_send()
        y_copy(t, 0).wait_send()
        y_copy(t, 1).wait_send()
    for j in range(last):
        aux_copy(j, False).wait_send()
        for c in range(chunks):
            line_copy(j, c).wait_send()


def body(points, assignment):
    owners = lax.axis_size("dev")
    rows, width = points.shape
    cap = 2 * rows // owners
    inner = 8
    outer = owners // inner
    chunk = width // 3 if width % (3 * LANES) == 0 else width
    chunks = width // chunk

    owner = assignment // CL_OWN
    local_label = assignment % CL_OWN
    matches = (owner[:, None] == jnp.arange(owners, dtype=jnp.int32)[None, :]).astype(jnp.float32)
    earlier = (jnp.arange(rows)[:, None] > jnp.arange(rows)[None, :]).astype(jnp.float32)
    before = jnp.dot(earlier, matches, preferred_element_type=jnp.float32)
    position = jnp.sum(before * matches, axis=1).astype(jnp.int32)
    seat = owner % inner
    place = owner - seat + seat % 2 * 4 + seat // 2 % 2 * 2 + seat // 4
    target = place * cap + position
    route = jnp.stack([target, local_label + 1])

    f32, b16 = jnp.float32, jnp.bfloat16
    dma = pltpu.SemaphoreType.DMA
    hops = max(outer - 1, 1)
    sums, aux = pl.pallas_call(
        functools.partial(kernel, inner, outer, cap, chunk),
        out_shape=(
            jax.ShapeDtypeStruct((CL_OWN, width), f32),
            jax.ShapeDtypeStruct((8, CL_OWN), f32),
        ),
        in_specs=[pl.BlockSpec(memory_space=pltpu.VMEM)] * 2,
        out_specs=[pl.BlockSpec(memory_space=pltpu.VMEM)] * 2,
        scratch_shapes=[
            pltpu.VMEM((rows, width), b16),
            pltpu.VMEM((rows, width), b16),
            pltpu.VMEM((8, rows), b16),
            pltpu.VMEM((CL_OWN, inner * LANES), b16),
            pltpu.VMEM((outer, chunks, inner // 2, 2, cap, chunk), f32),
            pltpu.VMEM((outer, chunks, inner // 2, cap, chunk), f32),
            pltpu.VMEM((outer, chunks, 2, 2, cap, chunk), f32),
            pltpu.VMEM((outer, chunks, 2, 2, cap, chunk), f32),
            pltpu.VMEM((inner, outer, 8, LANES), f32),
            pltpu.VMEM((inner, outer, 8, LANES), f32),
            pltpu.VMEM((hops, chunks, CL_OWN, chunk), f32),
            pltpu.VMEM((outer + 1, chunks, CL_OWN, chunk), f32),
            pltpu.VMEM((hops, 8, CL_OWN), f32),
            pltpu.VMEM((outer, 8, CL_OWN), f32),
            dma((inner,)), dma((inner,)),
            dma((outer, chunks)), dma((outer, chunks)),
            dma((outer, chunks)), dma((outer, chunks)),
            dma((outer, chunks, 2)), dma((outer, chunks, 2)),
            dma((hops, chunks)), dma((outer + 1, chunks)),
            dma((hops,)), dma((outer,)),
        ],
        compiler_params=pltpu.CompilerParams(
            collective_id=0, has_side_effects=True, vmem_limit_bytes=60 * 1024 * 1024
        ),
    )(points, route)
    counts = aux[0]
    squares = aux[1] + aux[2] + aux[3]
    sums, counts, squares = lax.psum((sums, counts, squares), "grp")
    return finish(sums, counts, squares)


def solution(mesh):
    return jax.shard_map(
        body,
        mesh=mesh,
        in_specs=(P(("grp", "dev"), None), P(("grp", "dev"))),
        out_specs=(P("dev", None), P("dev")),
        check_vma=False,
    )
```

profile of v0, /device:TPU:0, one launch (start us, length us, event | category | flops | bytes accessed | tf_op | source)
XLA Modules:
  0.0 94.3 jit_solution(15400862962733729939)
XLA Ops:
  0.6 0.7 add_select_fusion.6
  1.3 0.5 fusion.2
  1.9 0.7 fusion.10
  2.6 0.6 pad_add_fusion.route_ref
  3.2 87.5 %shard_map.41 = (f32[256,768]{1,0:T(8,128)}, f32[8,256]{1,0:T(8,128)}) custom-call(f32[1024,768]{1,0:T(8,128)} %points_ref.1, s32[2,1024]{1,0:T(2,128)} %pad_add_fusion.route_ref), custom_call_target="tpu_custom_call" | custom-call | tf_op jit(solution)/shard_map/pallas_call | solution.py:345
  90.7 0.9 slice_add_fusion
  91.5 2.1 %multiply_reduce_fusion = (f32[256]{0:T(256)S(1)}, f32[256,768]{1,0:T(8,128)}) fusion(f32[256,768]{1,0:T(8,128)} %get-tuple-element.4, f32[256]{0:T(256)S(1)} %bitcast.6), kind=kLoop, calls=%fused_computation.4 | loop fusion | flops 589568 | bytes 1574912 | tf_op jit(solution)/shard_map/reduce_sum | solution.py:18
  93.7 0.6 multiply_divide_fusion
where the time goes:
time: 94.5 us; the launch traced here: 94.3 us
  Pallas kernels  87.5 us (93%)
  other arithmetic  5.6 us (6%)
    pallas_call x1, Pallas kernels, body(): pl.pallas_call(functools.partial(kernel, inner, outer, cap, chunk), out_s...  87.5 us
    reduce_sum x1, other arithmetic, finish(): jnp.sum(sums * sums, axis=1) / denom  2.14 us

commit v1 on v0

v1 whole, which is shorter than its diff:
```python
import functools

import jax
import jax.numpy as jnp
from jax import lax
from jax.experimental import pallas as pl
from jax.experimental.pallas import tpu as pltpu
from jax.sharding import PartitionSpec as P

CL_OWN = 256
LANES = 128
INNER = 8
MESH = pl.DeviceIdType.MESH


def finish(sums, counts, squares):
    denom = jnp.maximum(counts, 1.0)
    centre = sums / denom[:, None]
    spread = (squares - jnp.sum(sums * sums, axis=1) / denom) / (denom * sums.shape[1])
    return (centre, spread)


def pieces(value, count):
    out = []
    for _ in range(count):
        part = value.astype(jnp.bfloat16)
        out.append(part)
        value = value - part.astype(jnp.float32)
    return out


def kernel(
    outer, cap, chunk, alone,
    points_ref, label_ref, main_ref, side_ref,
    stage, high, low, norm, facts, hit, hold, cout, xin, yin, mout, mgot, zout, zin, zaux, zin_aux,
    total, aux_all,
    lsem, msend, mrecv, csend, crecv, fsend, frecv, dsend, drecv, psend, precv,
    zsend, zrecv, asend, arecv, osem,
):
    inner = INNER
    me = lax.axis_index("dev")
    plane = me // inner
    seat = lax.rem(me, inner)
    rows, width = points_ref.shape
    owners = inner * outer
    chunks = width // chunk
    wide = chunk // 2
    rep = LANES // cap
    last = outer - 1
    rights, lefts = last - plane, plane
    steps = outer * chunks
    half = inner // 2 * cap
    ring = cout.shape[0]

    core = lax.rem(seat, 2)
    x = lax.rem(seat // 2, 2)
    y = seat // 4

    def target_plane(j):
        if j == last:
            return plane
        right_first = jnp.where(j < rights, last - j, j - rights)
        left_first = jnp.where(j < lefts, j, last - j + lefts)
        return jnp.where(rights > lefts, right_first, left_first)

    def fed(j):
        k = target_plane(j)
        return jnp.where(k > plane, plane > 0, plane < last)

    def across(d):
        other = 0
        for bit in range(3):
            own = lax.rem(seat // 2**bit, 2)
            other = other + (1 - own if d // 2**bit % 2 else own) * 2**bit
        return other

    def load(c):
        return pltpu.make_async_copy(
            points_ref.at[:, pl.ds(c * chunk, chunk)], stage.at[c], lsem.at[c]
        )

    def plane_copy(src, dst, ssem, rsem, d):
        return pltpu.make_async_remote_copy(
            src_ref=src,
            dst_ref=dst,
            send_sem=ssem,
            recv_sem=rsem,
            device_id={"dev": plane * inner + across(d)},
            device_id_type=MESH,
        )

    def core_copy(t):
        return plane_copy(
            cout.at[t % ring], hold.at[t, :, :, :, core], csend.at[t], crecv.at[t], 1
        )

    def core_arrival(t):
        return plane_copy(
            cout.at[t % ring], hold.at[t, :, :, :, 1 - core], csend.at[t], crecv.at[t], 1
        )

    def parts_of(t):
        return 2 if t == 0 else 1

    def first_copy(t, h, part):
        source = hold.at[t, 0, 1 - x] if h == 0 else hold.at[t, 1, :, 1 - y]
        target = xin.at[t, h]
        if parts_of(t) == 2:
            of = core if part == 0 else 1 - core
            source = hold.at[t, 0, 1 - x, :, of] if h == 0 else hold.at[t, 1, :, 1 - y, of]
            target = xin.at[t, h, :, of]
        return plane_copy(source, target, fsend.at[t, h, part], frecv.at[t, h, part], 2 if h == 0 else 4)

    def direct_copy(t, h):
        source = hold.at[t, 0, x, 1 - y] if h == 0 else hold.at[t, 1, 1 - x, y]
        return plane_copy(source, yin.at[t, h, 0], dsend.at[t, h], drecv.at[t, h], 4 if h == 0 else 2)

    def passed_copy(t, h):
        source = xin.at[t, 0, 1 - y] if h == 0 else xin.at[t, 1, 1 - x]
        return plane_copy(source, yin.at[t, h, 1], psend.at[t, h], precv.at[t, h], 4 if h == 0 else 2)

    def meta_copy(d, arriving):
        return plane_copy(
            mout.at[across(d)], mgot.at[across(d) if arriving else seat],
            msend.at[d], mrecv.at[d], d,
        )

    def line_copy(j, c):
        k = target_plane(j)
        step = jnp.where(k > plane, 1, -1)
        place = jnp.where(k == plane - 1, outer, k)
        return pltpu.make_async_remote_copy(
            src_ref=zout.at[j, c],
            dst_ref=zin.at[place, c],
            send_sem=zsend.at[j, c],
            recv_sem=zrecv.at[place, c],
            device_id={"dev": (plane + step) * inner + seat},
            device_id_type=MESH,
        )

    def line_arrival(place, c):
        side = jnp.where(plane > 0, -1, 1)
        return pltpu.make_async_remote_copy(
            src_ref=zout.at[0, c],
            dst_ref=zin.at[place, c],
            send_sem=zsend.at[0, c],
            recv_sem=zrecv.at[place, c],
            device_id={"dev": (plane + side) * inner + seat},
            device_id_type=MESH,
        )

    def aux_copy(j, arriving):
        k = target_plane(j)
        return pltpu.make_async_remote_copy(
            src_ref=zaux.at[j],
            dst_ref=zin_aux.at[k if arriving else plane],
            send_sem=asend.at[j],
            recv_sem=arecv.at[k if arriving else plane],
            device_id={"dev": k * inner + seat},
            device_id_type=MESH,
        )

    def route():
        label = label_ref[...]
        owner = lax.shift_right_logical(label, CL_OWN.bit_length() - 1)
        row = lax.broadcasted_iota(jnp.int32, (LANES, 2 * LANES), 0)
        col = lax.broadcasted_iota(jnp.int32, (LANES, 2 * LANES), 1)
        before = jnp.logical_or(row < col, col >= LANES).astype(jnp.bfloat16)
        index = lax.broadcasted_iota(jnp.int32, (owners, LANES), 0)
        blocks = rows // LANES
        marks = [
            (index == owner[:, b * LANES : (b + 1) * LANES]).astype(jnp.float32)
            for b in range(blocks)
        ]
        counts = jnp.dot(
            jnp.concatenate(marks, axis=0).astype(jnp.bfloat16), before,
            preferred_element_type=jnp.float32,
        )
        running = jnp.zeros((owners, LANES), jnp.float32)
        position = []
        for b in range(blocks):
            block = counts[b * owners : (b + 1) * owners]
            place = marks[b] * (block[:, :LANES] + running)
            position.append(jnp.sum(place, axis=0, keepdims=True))
            running = running + block[:, LANES:]
        position = jnp.concatenate(position, axis=1).astype(jnp.int32)
        inside = owner & (inner - 1)
        swapped = (inside & 1) * 4 + (lax.shift_right_logical(inside, 1) & 1) * 2
        swapped = swapped + lax.shift_right_logical(inside, 2)
        return (owner - inside + swapped) * cap + position

    def picks(j, target):
        row = lax.broadcasted_iota(jnp.int32, (2 * half, 1), 0)
        slot = target_plane(j) * (2 * half) + row
        slot = slot + jnp.where(row < half, core * half, -core * half)
        return (slot == target).astype(jnp.bfloat16)

    def split(c):
        load(c).wait()
        value = stage[c]
        top = value.astype(jnp.bfloat16)
        columns = slice(c * chunk, (c + 1) * chunk)
        high[:, columns] = top
        low[:, columns] = (value - top.astype(jnp.float32)).astype(jnp.bfloat16)
        square = value * value
        square = square[:, :wide] + square[:, wide:]
        if c == 0:
            norm[...] = square
        else:
            norm[...] += square

    def gather(t, pick):
        c = t % chunks
        columns = slice(c * chunk, (c + 1) * chunk)
        if t >= ring:
            core_copy(t - ring).wait_send()
        block = jnp.dot(pick, high[:, columns], preferred_element_type=jnp.float32)
        block = block + jnp.dot(pick, low[:, columns], preferred_element_type=jnp.float32)
        for h in range(2):
            part = block[:, h * wide : (h + 1) * wide]
            hold[t, h, :, :, core] = part[:half].reshape(2, 2, cap, wide)
            cout[t % ring, h] = part[half:].reshape(2, 2, cap, wide)

    def tell():
        norms = jnp.sum(norm[...].T, axis=0, keepdims=True)
        label = (label_ref[...] & (CL_OWN - 1)) + 1
        label = label.astype(jnp.float32).astype(jnp.bfloat16)
        blank = jnp.zeros((4, rows), jnp.bfloat16)
        facts[...] = jnp.concatenate([label] + pieces(norms, 3) + [blank], axis=0)

    def tell_slots(j, pick):
        told = lax.dot_general(
            facts[...], pick, (((1,), (1,)), ((), ())), preferred_element_type=jnp.float32
        )
        told = jnp.concatenate([told[0:1], told[1:2] + told[2:3] + told[3:4]], axis=0)
        for q in range(inner):
            p = q % 2 * 4 + q // 2 % 2 * 2 + (core if q < inner // 2 else 1 - core)
            mine = told[:, q * cap : (q + 1) * cap]
            mout[p, 2 * j : 2 * j + 2] = jnp.concatenate([mine] * rep, axis=1)

    lane = lax.broadcasted_iota(jnp.int32, (8, LANES), 1)
    line = lax.broadcasted_iota(jnp.int32, (8, LANES), 0)
    cluster = lax.broadcasted_iota(jnp.int32, (CL_OWN, LANES), 0).astype(jnp.float32) + 1.0

    def matches(j):
        if j == 0:
            for d in range(1, inner):
                meta_copy(d, True).wait_recv()
            mgot[seat] = mout[seat]
        weights = []
        for s in range(inner):
            block = mgot[across(s // 2 * 2) - core + s % 2, 2 * j : 2 * j + 2]
            hit[:, s * LANES : (s + 1) * LANES] = (cluster == block[0:1, :]).astype(jnp.bfloat16)
            weight = jnp.where(line == 0, 1.0, 0.0)
            for n, piece in enumerate(pieces(block[1:2, :], 3)):
                weight = jnp.where(line == n + 1, piece.astype(jnp.float32), weight)
            weights.append(jnp.where(lane < cap, weight, 0.0).astype(jnp.bfloat16))
        aux = lax.dot_general(
            jnp.concatenate(weights, axis=1), hit[...], (((1,), (1,)), ((), ())),
            preferred_element_type=jnp.float32,
        )
        if j < last:
            zaux[j] = aux
            aux_copy(j, False).start()
        else:
            aux_all[...] = aux

    def sources(t, h):
        own = hold.at[t, h, x, y]
        first = xin.at[t, h, y if h == 0 else x]
        direct, passed = yin.at[t, h, 0], yin.at[t, h, 1]
        return (own, first, direct, passed) if h == 0 else (own, direct, first, passed)

    def product(t, h, begin, end):
        stack = []
        for ref in sources(t, h)[begin:end]:
            for s in range(2):
                stack.extend(pieces(ref[s], rep))
        return jnp.dot(
            hit[:, begin * 2 * LANES : end * 2 * LANES], jnp.concatenate(stack, axis=0),
            preferred_element_type=jnp.float32,
        )

    def reduce(j, c):
        t = j * chunks + c
        for h in range(2):
            direct_copy(t, h).wait_recv()
        early = [product(t, h, 0, 3) for h in range(2)] if t == steps - 1 else None
        for h in range(2):
            passed_copy(t, h).wait_recv()
        for h in range(2):
            if early is None:
                value = product(t, h, 0, 4)
            else:
                value = early[h] + product(t, h, 3, 4)
            columns = slice(h * wide, (h + 1) * wide)
            if j < last:
                zout[j, c, :, columns] = value
            else:
                total[c, :, columns] = value

    def forward(j, c):
        @pl.when(fed(j))
        def _():
            line_arrival(target_plane(j), c).wait_recv()
            zout[j, c] += zin[target_plane(j), c]
            line_copy(j, c).start()

    def collect():
        for j in range(last):
            aux_copy(j, True).wait_recv()
            aux_all[...] += zin_aux[target_plane(j)]

    def settle(c):
        @pl.when(plane > 0)
        def _():
            line_arrival(plane, c).wait_recv()
            total[c] += zin[plane, c]

        @pl.when(plane < last)
        def _():
            line_arrival(outer, c).wait_recv()
            total[c] += zin[outer, c]

    def out_copy(c):
        return pltpu.make_async_copy(
            total.at[c], main_ref.at[:, pl.ds(c * chunk, chunk)], osem.at[c]
        )

    for d in range(chunks):
        load(d).start()
    barrier = pltpu.get_barrier_semaphore()
    for d in range(1, inner):
        peer = plane * inner + across(d)
        pl.semaphore_signal(barrier, inc=1, device_id={"dev": peer}, device_id_type=MESH)
    for d in range(1, outer):
        peer = lax.rem(plane + d, outer) * inner + seat
        pl.semaphore_signal(barrier, inc=1, device_id={"dev": peer}, device_id_type=MESH)

    target = route()
    pick = picks(0, target)
    split(0)
    gather(0, pick)
    pl.semaphore_wait(barrier, inner + outer - 2)
    for h in range(2):
        first_copy(0, h, 0).start()
    core_copy(0).start()
    ready = 1

    def prepare(pick):
        nonlocal ready
        t = ready
        if t < steps:
            if t < chunks:
                split(t)
            if t % chunks == 0:
                pick = picks(t // chunks, target)
            gather(t, pick)
            core_copy(t).start()
            ready += 1
        return pick

    pick = prepare(pick)
    core_arrival(0).wait_recv()
    for h in range(2):
        first_copy(0, h, 1).start()
    for h in range(2):
        direct_copy(0, h).start()
    pick = prepare(pick)
    core_arrival(1).wait_recv()
    for h in range(2):
        first_copy(1, h, 0).start()
    while ready < chunks:
        pick = prepare(pick)
    tell()
    for j in range(outer):
        tell_slots(j, picks(j, target))
    for d in range(1, inner):
        meta_copy(d, False).start()

    waiting = []

    def arrange(t):
        j, c = t // chunks, t % chunks
        if c == 0:
            matches(j)
        reduce(j, c)
        if j < last:
            @pl.when(jnp.logical_not(fed(j)))
            def _():
                line_copy(j, c).start()

            if j == last - 1:
                forward(j, c)
            else:
                waiting.append((j, c))
        while waiting and (len(waiting) > 2 or t >= last * chunks - 1):
            forward(*waiting.pop(0))

    for t in range(steps):
        for h in range(2):
            for part in range(parts_of(t)):
                first_copy(t, h, part).wait_recv()
            passed_copy(t, h).start()
        if t + 2 < steps:
            core_arrival(t + 2).wait_recv()
            for h in range(2):
                first_copy(t + 2, h, 0).start()
        if t + 1 < steps:
            for h in range(2):
                direct_copy(t + 1, h).start()
        pick = prepare(pick)
        if t > 0:
            arrange(t - 1)

    collect()
    for c in range(chunks):
        if c == chunks - 1:
            arrange(steps - 1)
        settle(c)
        if not alone:
            out_copy(c).start()
    if alone:
        counts = jnp.maximum(aux_all[0:1, :], 1.0)
        denom = jnp.broadcast_to(counts, (LANES, CL_OWN)).T
        gathered = jnp.zeros((CL_OWN, LANES), jnp.float32)
        for c in range(chunks):
            for n in range(chunk // LANES):
                columns = slice(n * LANES, (n + 1) * LANES)
                value = total[c, :, columns]
                gathered = gathered + value * value
                total[c, :, columns] = value / denom
            out_copy(c).start()
        lengths = jnp.sum(gathered.T, axis=0, keepdims=True)
        squares = aux_all[1:2, :] + aux_all[2:3, :] + aux_all[3:4, :]
        side_ref[...] = (squares - lengths / counts) / (counts * width)
    else:
        side_ref[...] = aux_all[...]

    for d in range(1, inner):
        meta_copy(d, False).wait_send()
    for t in range(steps):
        if t >= steps - ring:
            core_copy(t).wait_send()
        for h in range(2):
            for part in range(parts_of(t)):
                first_copy(t, h, part).wait_send()
            direct_copy(t, h).wait_send()
            passed_copy(t, h).wait_send()
    for j in range(last):
        aux_copy(j, False).wait_send()
        for c in range(chunks):
            line_copy(j, c).wait_send()
    for c in range(chunks):
        out_copy(c).wait()


def body(points, assignment):
    owners = lax.axis_size("dev")
    alone = lax.axis_size("grp") == 1
    rows, width = points.shape
    cap = 2 * rows // owners
    outer = owners // INNER
    chunk = 2 * LANES
    chunks = width // chunk
    wide = chunk // 2
    steps = outer * chunks
    ring = min(steps, 4)

    f32, b16 = jnp.float32, jnp.bfloat16
    dma = pltpu.SemaphoreType.DMA
    hops = max(outer - 1, 1)
    side = (1, CL_OWN) if alone else (8, CL_OWN)
    vmem = pl.BlockSpec(memory_space=pltpu.VMEM)
    hbm = pl.BlockSpec(memory_space=pltpu.HBM)
    main, side = pl.pallas_call(
        functools.partial(kernel, outer, cap, chunk, alone),
        out_shape=(
            jax.ShapeDtypeStruct((CL_OWN, width), f32),
            jax.ShapeDtypeStruct(side, f32),
        ),
        in_specs=[hbm, vmem],
        out_specs=[hbm, vmem],
        scratch_shapes=[
            pltpu.VMEM((chunks, rows, chunk), f32),
            pltpu.VMEM((rows, width), b16),
            pltpu.VMEM((rows, width), b16),
            pltpu.VMEM((rows, LANES), f32),
            pltpu.VMEM((8, rows), b16),
            pltpu.VMEM((CL_OWN, INNER * LANES), b16),
            pltpu.VMEM((steps, 2, 2, 2, 2, cap, wide), f32),
            pltpu.VMEM((ring, 2, 2, 2, cap, wide), f32),
            pltpu.VMEM((steps, 2, 2, 2, cap, wide), f32),
            pltpu.VMEM((steps, 2, 2, 2, cap, wide), f32),
            pltpu.VMEM((INNER, 2 * outer, LANES), f32),
            pltpu.VMEM((INNER, 2 * outer, LANES), f32),
            pltpu.VMEM((hops, chunks, CL_OWN, chunk), f32),
            pltpu.VMEM((outer + 1, chunks, CL_OWN, chunk), f32),
            pltpu.VMEM((hops, 8, CL_OWN), f32),
            pltpu.VMEM((outer, 8, CL_OWN), f32),
            pltpu.VMEM((chunks, CL_OWN, chunk), f32),
            pltpu.VMEM((8, CL_OWN), f32),
            dma((chunks,)),
            dma((INNER,)), dma((INNER,)),
            dma((steps,)), dma((steps,)),
            dma((steps, 2, 2)), dma((steps, 2, 2)),
            dma((steps, 2)), dma((steps, 2)),
            dma((steps, 2)), dma((steps, 2)),
            dma((hops, chunks)), dma((outer + 1, chunks)),
            dma((hops,)), dma((outer,)),
            dma((chunks,)),
        ],
        compiler_params=pltpu.CompilerParams(
            collective_id=0, has_side_effects=True, vmem_limit_bytes=63 * 1024 * 1024
        ),
    )(points, assignment.reshape(1, rows))
    if alone:
        return main, side[0]
    squares = side[1] + side[2] + side[3]
    sums, counts, squares = lax.psum((main, side[0], squares), "grp")
    return finish(sums, counts, squares)


def solution(mesh):
    return jax.shard_map(
        body,
        mesh=mesh,
        in_specs=(P(("grp", "dev"), None), P(("grp", "dev"))),
        out_specs=(P("dev", None), P("dev")),
        check_vma=False,
    )
```

time: 94.5 us -> 84.7 us (0.90)
  Pallas kernels: 87.5 us -> 80.5 us
  other arithmetic: 5.6 us -> 0 us
  local copies, waits for them, and re-layouts: 0 us -> 3.29 us
    pallas_call x1, Pallas kernels: 87.5 us -> 80.5 us  [body(): pl.pallas_call(functools.partial(kernel, outer, cap, chunk, alone), out_s...]
    unnamed x0 -> x2, local copies, waits for them, and re-layouts: none -> 3.29 us
    reduce_sum x1 -> x0, other arithmetic: 2.14 us -> none  [finish(): jnp.sum(sums * sums, axis=1) / denom]
    add x2 -> x0, other arithmetic: 1.58 us -> none  [the longest x1 0.85 us: body(): squares = aux[1] + aux[2] + aux[3]]
where the time goes in v1:
time: 84.7 us; the launch traced here: 84.5 us
  Pallas kernels  80.5 us (95%)
  local copies, waits for them, and re-layouts  3.29 us (4%)
    pallas_call x1, Pallas kernels, body(): pl.pallas_call(functools.partial(kernel, outer, cap, chunk, alone), out_s...  80.5 us
    unnamed x2, local copies, waits for them, and re-layouts  3.29 us

profile of v1, /device:TPU:0, one launch (start us, length us, event | category | flops | bytes accessed | tf_op | source)
XLA Modules:
  0.0 84.5 jit_solution(3403878788162721314)
XLA Ops:
  0.6 80.5 %shard_map.41 = (f32[256,768]{1,0:T(8,128)}, f32[1,256]{1,0:T(1,128)}) custom-call(f32[1024,768]{1,0:T(8,128)} %points_ref.1, s32[1,1024]{1,0:T(1,128)} %bitcast.2), custom_call_target="tpu_custom_call" | custom-call | tf_op jit(solution)/shard_map/pallas_call | solution.py:476
  81.2 2.1 %copy.6 = f32[256,768]{1,0:T(8,128)} copy(f32[256,768]{1,0:T(8,128)} %get-tuple-element.8) | data formatting | bytes 1572864
  83.2 1.2 %copy.7 = f32[256]{0:T(256)} copy(f32[256]{0:T(256)} %bitcast.3) | data formatting | bytes 2048

commit v2 on v1

--- a/solution.py
+++ b/solution.py
@@ -10,6 +10,7 @@
 CL_OWN = 256
 LANES = 128
 INNER = 8
+LIMIT = 52 * 1024 * 1024
 MESH = pl.DeviceIdType.MESH
 
 
@@ -31,11 +32,11 @@
 
 def kernel(
     outer, cap, chunk, alone,
-    points_ref, label_ref, main_ref, side_ref,
-    stage, high, low, norm, facts, hit, hold, cout, xin, yin, mout, mgot, zout, zin, zaux, zin_aux,
-    total, aux_all,
-    lsem, msend, mrecv, csend, crecv, fsend, frecv, dsend, drecv, psend, precv,
-    zsend, zrecv, asend, arecv, osem,
+    points_ref, label_hbm, main_ref, side_ref,
+    label_ref, stage, high, low, norm, facts, hit, hold, cout, xin, yin, mout, mgot, zout, zin, zaux, zin_aux,
+    total, aux_all, inverse, lengths,
+    lsem, msend, mrecv, csend, crecv, fsend, frecv, ysend, yrecv,
+    zsend, zrecv, asend, arecv,
 ):
     inner = INNER
     me = lax.axis_index("dev")
@@ -74,10 +75,16 @@
             other = other + (1 - own if d // 2**bit % 2 else own) * 2**bit
         return other
 
+    def load_label():
+        return pltpu.make_async_copy(label_hbm, label_ref, lsem.at[chunks])
+
     def load(c):
         return pltpu.make_async_copy(
             points_ref.at[:, pl.ds(c * chunk, chunk)], stage.at[c], lsem.at[c]
         )
+
+    def drain(ref, sem):
+        pltpu.make_async_copy(ref, ref, sem).wait()
 
     def plane_copy(src, dst, ssem, rsem, d):
         return pltpu.make_async_remote_copy(
@@ -91,16 +98,16 @@
 
     def core_copy(t):
         return plane_copy(
-            cout.at[t % ring], hold.at[t, :, :, :, core], csend.at[t], crecv.at[t], 1
+            cout.at[t % ring], hold.at[t, :, :, :, core], csend.at[t % ring], crecv.at[t], 1
         )
 
     def core_arrival(t):
         return plane_copy(
-            cout.at[t % ring], hold.at[t, :, :, :, 1 - core], csend.at[t], crecv.at[t], 1
+            cout.at[t % ring], hold.at[t, :, :, :, 1 - core], csend.at[t % ring], crecv.at[t], 1
         )
 
     def parts_of(t):
-        return 2 if t == 0 else 1
+        return 2 if t < 2 else 1
 
     def first_copy(t, h, part):
         source = hold.at[t, 0, 1 - x] if h == 0 else hold.at[t, 1, :, 1 - y]
@@ -109,21 +116,19 @@
             of = core if part == 0 else 1 - core
             source = hold.at[t, 0, 1 - x, :, of] if h == 0 else hold.at[t, 1, :, 1 - y, of]
             target = xin.at[t, h, :, of]
-        return plane_copy(source, target, fsend.at[t, h, part], frecv.at[t, h, part], 2 if h == 0 else 4)
+        return plane_copy(source, target, fsend, frecv.at[t], 2 if h == 0 else 4)
 
     def direct_copy(t, h):
         source = hold.at[t, 0, x, 1 - y] if h == 0 else hold.at[t, 1, 1 - x, y]
-        return plane_copy(source, yin.at[t, h, 0], dsend.at[t, h], drecv.at[t, h], 4 if h == 0 else 2)
+        arrived = yrecv.at[steps if t == steps - 1 else t]
+        return plane_copy(source, yin.at[t, h, 0], ysend, arrived, 4 if h == 0 else 2)
 
     def passed_copy(t, h):
         source = xin.at[t, 0, 1 - y] if h == 0 else xin.at[t, 1, 1 - x]
-        return plane_copy(source, yin.at[t, h, 1], psend.at[t, h], precv.at[t, h], 4 if h == 0 else 2)
-
-    def meta_copy(d, arriving):
-        return plane_copy(
-            mout.at[across(d)], mgot.at[across(d) if arriving else seat],
-            msend.at[d], mrecv.at[d], d,
-        )
+        return plane_copy(source, yin.at[t, h, 1], ysend, yrecv.at[t], 4 if h == 0 else 2)
+
+    def meta_copy(d):
+        return plane_copy(mout.at[across(d)], mgot.at[seat], msend, mrecv, d)
 
     def line_copy(j, c):
         k = target_plane(j)
@@ -132,7 +137,7 @@
         return pltpu.make_async_remote_copy(
             src_ref=zout.at[j, c],
             dst_ref=zin.at[place, c],
-            send_sem=zsend.at[j, c],
+            send_sem=zsend,
             recv_sem=zrecv.at[place, c],
             device_id={"dev": (plane + step) * inner + seat},
             device_id_type=MESH,
@@ -143,24 +148,24 @@
         return pltpu.make_async_remote_copy(
             src_ref=zout.at[0, c],
             dst_ref=zin.at[place, c],
-            send_sem=zsend.at[0, c],
+            send_sem=zsend,
             recv_sem=zrecv.at[place, c],
             device_id={"dev": (plane + side) * inner + seat},
             device_id_type=MESH,
         )
 
-    def aux_copy(j, arriving):
-        k = target_plane(j)
+    def aux_copy(j):
         return pltpu.make_async_remote_copy(
             src_ref=zaux.at[j],
-            dst_ref=zin_aux.at[k if arriving else plane],
-            send_sem=asend.at[j],
-            recv_sem=arecv.at[k if arriving else plane],
-            device_id={"dev": k * inner + seat},
+            dst_ref=zin_aux.at[plane],
+            send_sem=asend,
+            recv_sem=arecv,
+            device_id={"dev": target_plane(j) * inner + seat},
             device_id_type=MESH,
         )
 
     def route():
+        load_label().wait()
         label = label_ref[...]
         owner = lax.shift_right_logical(label, CL_OWN.bit_length() - 1)
         row = lax.broadcasted_iota(jnp.int32, (LANES, 2 * LANES), 0)
@@ -209,17 +214,20 @@
         else:
             norm[...] += square
 
-    def gather(t, pick):
+    def gather(t, pick, begin=0, end=2 * half):
         c = t % chunks
         columns = slice(c * chunk, (c + 1) * chunk)
-        if t >= ring:
+        if t >= ring and end > half:
             core_copy(t - ring).wait_send()
-        block = jnp.dot(pick, high[:, columns], preferred_element_type=jnp.float32)
-        block = block + jnp.dot(pick, low[:, columns], preferred_element_type=jnp.float32)
+        rows_of = pick[begin:end]
+        block = jnp.dot(rows_of, high[:, columns], preferred_element_type=jnp.float32)
+        block = block + jnp.dot(rows_of, low[:, columns], preferred_element_type=jnp.float32)
         for h in range(2):
             part = block[:, h * wide : (h + 1) * wide]
-            hold[t, h, :, :, core] = part[:half].reshape(2, 2, cap, wide)
-            cout[t % ring, h] = part[half:].reshape(2, 2, cap, wide)
+            if begin == 0:
+                hold[t, h, :, :, core] = part[:half].reshape(2, 2, cap, wide)
+            if end > half:
+                cout[t % ring, h] = part[half - begin :].reshape(2, 2, cap, wide)
 
     def tell():
         norms = jnp.sum(norm[...].T, axis=0, keepdims=True)
@@ -244,8 +252,7 @@
 
     def matches(j):
         if j == 0:
-            for d in range(1, inner):
-                meta_copy(d, True).wait_recv()
+            drain(mgot.at[pl.ds(0, inner - 1)], mrecv)
             mgot[seat] = mout[seat]
         weights = []
         for s in range(inner):
@@ -261,7 +268,7 @@
         )
         if j < last:
             zaux[j] = aux
-            aux_copy(j, False).start()
+            aux_copy(j).start()
         else:
             aux_all[...] = aux
 
@@ -283,21 +290,45 @@
 
     def reduce(j, c):
         t = j * chunks + c
+        drain(yin.at[t], yrecv.at[t])
         for h in range(2):
-            direct_copy(t, h).wait_recv()
-        early = [product(t, h, 0, 3) for h in range(2)] if t == steps - 1 else None
+            zout[j, c, :, h * wide : (h + 1) * wide] = product(t, h, 0, 4)
+
+    def conclude(c):
+        t = last * chunks + c
+        final = t == steps - 1
+        if final:
+            drain(yin.at[t, :, 0], yrecv.at[steps])
+        else:
+            drain(yin.at[t], yrecv.at[t])
         for h in range(2):
-            passed_copy(t, h).wait_recv()
+            total[c, :, h * wide : (h + 1) * wide] = product(t, h, 0, 3 if final else 4)
+
+        @pl.when(plane > 0)
+        def _():
+            line_arrival(plane, c).wait_recv()
+            total[c] += zin[plane, c]
+
+        @pl.when(plane < last)
+        def _():
+            line_arrival(outer, c).wait_recv()
+            total[c] += zin[outer, c]
+
+        if final:
+            drain(yin.at[t, :, 1], yrecv.at[t])
         for h in range(2):
-            if early is None:
-                value = product(t, h, 0, 4)
-            else:
-                value = early[h] + product(t, h, 3, 4)
-            columns = slice(h * wide, (h + 1) * wide)
-            if j < last:
-                zout[j, c, :, columns] = value
-            else:
-                total[c, :, columns] = value
+            begin = c * chunk + h * wide
+            value = total[c, :, h * wide : (h + 1) * wide]
+            if final:
+                value = value + product(t, h, 3, 4)
+            if alone:
+                square = value * value
+                if c == 0 and h == 0:
+                    lengths[...] = square
+                else:
+                    lengths[...] += square
+                value = value * inverse[...]
+            main_ref[:, begin : begin + wide] = value
 
     def forward(j, c):
         @pl.when(fed(j))
@@ -307,28 +338,16 @@
             line_copy(j, c).start()
 
     def collect():
+        if last:
+            drain(zin_aux.at[pl.ds(0, last)], arecv)
         for j in range(last):
-            aux_copy(j, True).wait_recv()
             aux_all[...] += zin_aux[target_plane(j)]
-
-    def settle(c):
-        @pl.when(plane > 0)
-        def _():
-            line_arrival(plane, c).wait_recv()
-            total[c] += zin[plane, c]
-
-        @pl.when(plane < last)
-        def _():
-            line_arrival(outer, c).wait_recv()
-            total[c] += zin[outer, c]
-
-    def out_copy(c):
-        return pltpu.make_async_copy(
-            total.at[c], main_ref.at[:, pl.ds(c * chunk, chunk)], osem.at[c]
-        )
-
-    for d in range(chunks):
-        load(d).start()
+        if alone:
+            denom = jnp.maximum(aux_all[0:1, :], 1.0)
+            inverse[...] = 1.0 / jnp.broadcast_to(denom, (LANES, CL_OWN)).T
+
+    load_label().start()
+    load(0).start()
     barrier = pltpu.get_barrier_semaphore()
     for d in range(1, inner):
         peer = plane * inner + across(d)
@@ -340,10 +359,13 @@
     target = route()
     pick = picks(0, target)
     split(0)
-    gather(0, pick)
+    for c in range(1, chunks):
+        load(c).start()
+    gather(0, pick, 0, half)
     pl.semaphore_wait(barrier, inner + outer - 2)
     for h in range(2):
         first_copy(0, h, 0).start()
+    gather(0, pick, half, 2 * half)
     core_copy(0).start()
     ready = 1
 
@@ -360,7 +382,13 @@
             ready += 1
         return pick
 
-    pick = prepare(pick)
+    split(1)
+    gather(1, pick, 0, half)
+    for h in range(2):
+        first_copy(1, h, 0).start()
+    gather(1, pick, half, 2 * half)
+    core_copy(1).start()
+    ready = 2
     core_arrival(0).wait_recv()
     for h in range(2):
         first_copy(0, h, 1).start()
@@ -369,14 +397,14 @@
     pick = prepare(pick)
     core_arrival(1).wait_recv()
     for h in range(2):
-        first_copy(1, h, 0).start()
+        first_copy(1, h, 1).start()
     while ready < chunks:
         pick = prepare(pick)
     tell()
     for j in range(outer):
         tell_slots(j, picks(j, target))
     for d in range(1, inner):
-        meta_copy(d, False).start()
+        meta_copy(d).start()
 
     waiting = []
 
@@ -384,8 +412,13 @@
         j, c = t // chunks, t % chunks
         if c == 0:
             matches(j)
-        reduce(j, c)
-        if j < last:
+        if j == last:
+            if c == 0:
+                collect()
+            conclude(c)
+        else:
+            reduce(j, c)
+
             @pl.when(jnp.logical_not(fed(j)))
             def _():
                 line_copy(j, c).start()
@@ -398,9 +431,8 @@
             forward(*waiting.pop(0))
 
     for t in range(steps):
+        drain(xin.at[t], frecv.at[t])
         for h in range(2):
-            for part in range(parts_of(t)):
-                first_copy(t, h, part).wait_recv()
             passed_copy(t, h).start()
         if t + 2 < steps:
             core_arrival(t + 2).wait_recv()
@@ -413,46 +445,23 @@
         if t > 0:
             arrange(t - 1)
 
-    collect()
-    for c in range(chunks):
-        if c == chunks - 1:
-            arrange(steps - 1)
-        settle(c)
-        if not alone:
-            out_copy(c).start()
+    arrange(steps - 1)
     if alone:
-        counts = jnp.maximum(aux_all[0:1, :], 1.0)
-        denom = jnp.broadcast_to(counts, (LANES, CL_OWN)).T
-        gathered = jnp.zeros((CL_OWN, LANES), jnp.float32)
-        for c in range(chunks):
-            for n in range(chunk // LANES):
-                columns = slice(n * LANES, (n + 1) * LANES)
-                value = total[c, :, columns]
-                gathered = gathered + value * value
-                total[c, :, columns] = value / denom
-            out_copy(c).start()
-        lengths = jnp.sum(gathered.T, axis=0, keepdims=True)
+        denom = jnp.maximum(aux_all[0:1, :], 1.0)
         squares = aux_all[1:2, :] + aux_all[2:3, :] + aux_all[3:4, :]
-        side_ref[...] = (squares - lengths / counts) / (counts * width)
+        length = jnp.sum(lengths[...].T, axis=0, keepdims=True)
+        side_ref[...] = (squares - length / denom) / (denom * width)
     else:
         side_ref[...] = aux_all[...]
 
-    for d in range(1, inner):
-        meta_copy(d, False).wait_send()
-    for t in range(steps):
-        if t >= steps - ring:
-            core_copy(t).wait_send()
-        for h in range(2):
-            for part in range(parts_of(t)):
-                first_copy(t, h, part).wait_send()
-            direct_copy(t, h).wait_send()
-            passed_copy(t, h).wait_send()
-    for j in range(last):
-        aux_copy(j, False).wait_send()
-        for c in range(chunks):
-            line_copy(j, c).wait_send()
-    for c in range(chunks):
-        out_copy(c).wait()
+    drain(mout.at[pl.ds(0, inner - 1)], msend)
+    for t in range(max(steps - ring, 0), steps):
+        core_copy(t).wait_send()
+    drain(xin, fsend)
+    drain(yin, ysend)
+    if last:
+        drain(zout, zsend)
+        drain(zaux, asend)
 
 
 def body(points, assignment):
@@ -479,9 +488,10 @@
             jax.ShapeDtypeStruct((CL_OWN, width), f32),
             jax.ShapeDtypeStruct(side, f32),
         ),
-        in_specs=[hbm, vmem],
-        out_specs=[hbm, vmem],
+        in_specs=[hbm, hbm],
+        out_specs=[vmem, vmem],
         scratch_shapes=[
+            pltpu.VMEM((1, rows), jnp.int32),
             pltpu.VMEM((chunks, rows, chunk), f32),
             pltpu.VMEM((rows, width), b16),
             pltpu.VMEM((rows, width), b16),
@@ -500,20 +510,20 @@
             pltpu.VMEM((outer, 8, CL_OWN), f32),
             pltpu.VMEM((chunks, CL_OWN, chunk), f32),
             pltpu.VMEM((8, CL_OWN), f32),
-            dma((chunks,)),
-            dma((INNER,)), dma((INNER,)),
-            dma((steps,)), dma((steps,)),
-            dma((steps, 2, 2)), dma((steps, 2, 2)),
-            dma((steps, 2)), dma((steps, 2)),
-            dma((steps, 2)), dma((steps, 2)),
-            dma((hops, chunks)), dma((outer + 1, chunks)),
-            dma((hops,)), dma((outer,)),
-            dma((chunks,)),
+            pltpu.VMEM((CL_OWN, LANES), f32),
+            pltpu.VMEM((CL_OWN, LANES), f32),
+            dma((chunks + 1,)),
+            dma(()), dma(()),
+            dma((ring,)), dma((steps,)),
+            dma(()), dma((steps,)),
+            dma(()), dma((steps + 1,)),
+            dma(()), dma((outer + 1, chunks)),
+            dma(()), dma(()),
         ],
         compiler_params=pltpu.CompilerParams(
-            collective_id=0, has_side_effects=True, vmem_limit_bytes=63 * 1024 * 1024
+            collective_id=0, has_side_effects=True, vmem_limit_bytes=LIMIT
         ),
-    )(points, assignment.reshape(1, rows))
+    )(points, pltpu.with_memory_space_constraint(assignment.reshape(1, rows), pltpu.HBM))
     if alone:
         return main, side[0]
     squares = side[1] + side[2] + side[3]

time: 84.7 us -> 78.5 us (0.927)
  Pallas kernels: 80.5 us -> 76.2 us
  local copies, waits for them, and re-layouts: 3.29 us -> 1.44 us
    pallas_call x1, Pallas kernels: 80.5 us -> 76.2 us  [body(): pl.pallas_call(functools.partial(kernel, outer, cap, chunk, alone), out_s...]
    unnamed x2, local copies, waits for them, and re-layouts: 3.29 us -> 1.44 us
where the time goes in v2:
time: 78.5 us; the launch traced here: 78.3 us
  Pallas kernels  76.2 us (97%)
  local copies, waits for them, and re-layouts  1.44 us (2%)
    pallas_call x1, Pallas kernels, body(): pl.pallas_call(functools.partial(kernel, outer, cap, chunk, alone), out_s...  76.2 us

profile of v2, /device:TPU:0, one launch (start us, length us, event | category | flops | bytes accessed | tf_op | source)
XLA Modules:
  0.0 78.3 jit_solution(14720589375657664467)
XLA Ops:
  0.6 76.2 %shard_map.41 = (f32[256,768]{1,0:T(8,128)S(1)}, f32[1,256]{1,0:T(1,128)S(1)}) custom-call(f32[1024,768]{1,0:T(8,128)} %points_ref.1, s32[1,1024]{1,0:T(1,128)} %bitcast.3), custom_call_target="tpu_custom_call" | custom-call | tf_op jit(solution)/shard_map/pallas_call | solution.py:485
  76.8 0.9 %copy.6 = f32[256,768]{1,0:T(8,128)} copy(f32[256,768]{1,0:T(8,128)S(1)} %get-tuple-element.8) | data formatting | bytes 1572864
  77.7 0.6 copy.7

commit v3 on v2

--- a/solution.py
+++ b/solution.py
@@ -31,12 +31,12 @@
 
 
 def kernel(
-    outer, cap, chunk, alone,
+    outer, cap, chunk, alone, paired,
     points_ref, label_hbm, main_ref, side_ref,
     label_ref, stage, high, low, norm, facts, hit, hold, cout, xin, yin, mout, mgot, zout, zin, zaux, zin_aux,
     total, aux_all, inverse, lengths,
     lsem, msend, mrecv, csend, crecv, fsend, frecv, ysend, yrecv,
-    zsend, zrecv, asend, arecv,
+    zsend, zrecv, asend, arecv, *extra,
 ):
     inner = INNER
     me = lax.axis_index("dev")
@@ -44,7 +44,8 @@
     seat = lax.rem(me, inner)
     rows, width = points_ref.shape
     owners = inner * outer
-    chunks = width // chunk
+    shift = 1 if paired else 0
+    chunks = width // chunk - shift
     wide = chunk // 2
     rep = LANES // cap
     last = outer - 1
@@ -52,6 +53,13 @@
     steps = outer * chunks
     half = inner // 2 * cap
     ring = cout.shape[0]
+    if paired:
+        (
+            zlabel, zraw, zhigh, zlow, zfacts, zhold, zcout, zxin, zsout, zsin,
+            zzout, zzin, zzown, zmout, zmgot, zhit,
+            lssem, lrsem, rssem, rrsem, xcsend, xcrecv, xfsend, xfrecv,
+            xssend, xsrecv, zzsend, zzrecv, zmsend, zmrecv,
+        ) = extra
 
     core = lax.rem(seat, 2)
     x = lax.rem(seat // 2, 2)
@@ -76,7 +84,7 @@
         return other
 
     def load_label():
-        return pltpu.make_async_copy(label_hbm, label_ref, lsem.at[chunks])
+        return pltpu.make_async_copy(label_hbm, label_ref, lsem.at[width // chunk])
 
     def load(c):
         return pltpu.make_async_copy(
@@ -164,9 +172,7 @@
             device_id_type=MESH,
         )
 
-    def route():
-        load_label().wait()
-        label = label_ref[...]
+    def route(label):
         owner = lax.shift_right_logical(label, CL_OWN.bit_length() - 1)
         row = lax.broadcasted_iota(jnp.int32, (LANES, 2 * LANES), 0)
         col = lax.broadcasted_iota(jnp.int32, (LANES, 2 * LANES), 1)
@@ -194,9 +200,9 @@
         swapped = swapped + lax.shift_right_logical(inside, 2)
         return (owner - inside + swapped) * cap + position
 
-    def picks(j, target):
+    def picks(k, target):
         row = lax.broadcasted_iota(jnp.int32, (2 * half, 1), 0)
-        slot = target_plane(j) * (2 * half) + row
+        slot = k * (2 * half) + row
         slot = slot + jnp.where(row < half, core * half, -core * half)
         return (slot == target).astype(jnp.bfloat16)
 
@@ -209,13 +215,13 @@
         low[:, columns] = (value - top.astype(jnp.float32)).astype(jnp.bfloat16)
         square = value * value
         square = square[:, :wide] + square[:, wide:]
-        if c == 0:
+        if c == shift:
             norm[...] = square
         else:
             norm[...] += square
 
     def gather(t, pick, begin=0, end=2 * half):
-        c = t % chunks
+        c = t % chunks + shift
         columns = slice(c * chunk, (c + 1) * chunk)
         if t >= ring and end > half:
             core_copy(t - ring).wait_send()
@@ -229,10 +235,12 @@
             if end > half:
                 cout[t % ring, h] = part[half - begin :].reshape(2, 2, cap, wide)
 
+    def inside_label(label):
+        return ((label & (CL_OWN - 1)) + 1).astype(jnp.float32).astype(jnp.bfloat16)
+
     def tell():
         norms = jnp.sum(norm[...].T, axis=0, keepdims=True)
-        label = (label_ref[...] & (CL_OWN - 1)) + 1
-        label = label.astype(jnp.float32).astype(jnp.bfloat16)
+        label = inside_label(label_ref[...])
         blank = jnp.zeros((4, rows), jnp.bfloat16)
         facts[...] = jnp.concatenate([label] + pieces(norms, 3) + [blank], axis=0)
 
@@ -317,7 +325,7 @@
         if final:
             drain(yin.at[t, :, 1], yrecv.at[t])
         for h in range(2):
-            begin = c * chunk + h * wide
+            begin = (c + shift) * chunk + h * wide
             value = total[c, :, h * wide : (h + 1) * wide]
             if final:
                 value = value + product(t, h, 3, 4)
@@ -346,8 +354,138 @@
             denom = jnp.maximum(aux_all[0:1, :], 1.0)
             inverse[...] = 1.0 / jnp.broadcast_to(denom, (LANES, CL_OWN)).T
 
+    def pair_copy(src, dst, ssem, rsem):
+        return pltpu.make_async_remote_copy(
+            src_ref=src,
+            dst_ref=dst,
+            send_sem=ssem,
+            recv_sem=rsem,
+            device_id={"dev": (plane + 1 - 2 * lax.rem(plane, 2)) * inner + seat},
+            device_id_type=MESH,
+        )
+
+    def pair_label():
+        return pair_copy(label_hbm, zlabel, lssem, lrsem)
+
+    def pair_rows():
+        return pair_copy(points_ref.at[:, pl.ds(0, chunk)], zraw, rssem, rrsem)
+
+    def pair_plane(m):
+        return lax.rem(plane + 2, outer) if m == 0 else plane
+
+    def pair_tell(pair_target):
+        zfacts[...] = jnp.concatenate(
+            [inside_label(zlabel[...]), jnp.zeros((7, rows), jnp.bfloat16)], axis=0
+        )
+        for m in range(2):
+            for zs, (fact, slots) in enumerate(((facts, target), (zfacts, pair_target))):
+                told = lax.dot_general(
+                    fact[...], picks(pair_plane(m), slots), (((1,), (1,)), ((), ())),
+                    preferred_element_type=jnp.float32,
+                )
+                for side in range(2):
+                    for xx in range(2):
+                        row = m * 4 + zs * 2 + xx
+                        begin = side * half + xx * LANES
+                        zmout[side, row : row + 1] = told[0:1, begin : begin + LANES]
+        zmgot[core] = zmout[0]
+        for d in range(1, 6):
+            plane_copy(zmout.at[d % 2], zmgot.at[d // 2 * 2 + core], zmsend, zmrecv, d).start()
+
+    def pair_core(m, zs):
+        return plane_copy(
+            zcout.at[m, zs], zhold.at[m, :, :, :, zs * 2 + core], xcsend, xcrecv.at[m], 1
+        )
+
+    def pair_first(m, h):
+        source = zhold.at[m, 0, 1 - x] if h == 0 else zhold.at[m, 1, :, 1 - y]
+        return plane_copy(source, zxin.at[m, h], xfsend, xfrecv.at[m], 2 if h == 0 else 4)
+
+    def pair_sums(m, h):
+        return plane_copy(
+            zsout.at[m, h], zsin.at[m, h], xssend, xsrecv.at[m], 4 if h == 0 else 2
+        )
+
+    def pair_line():
+        return pltpu.make_async_remote_copy(
+            src_ref=zzout,
+            dst_ref=zzin,
+            send_sem=zzsend,
+            recv_sem=zzrecv,
+            device_id={"dev": pair_plane(0) * inner + seat},
+            device_id_type=MESH,
+        )
+
+    def pair_gather(m, pair_target):
+        if m == 0:
+            pair_rows().wait_recv()
+            value = zraw[...]
+            top = value.astype(jnp.bfloat16)
+            zhigh[...] = top
+            zlow[...] = (value - top.astype(jnp.float32)).astype(jnp.bfloat16)
+        for zs in range(2):
+            pick = picks(pair_plane(m), pair_target if zs else target)
+            upper = zhigh[...] if zs else high[:, :chunk]
+            lower = zlow[...] if zs else low[:, :chunk]
+            block = jnp.dot(pick, upper, preferred_element_type=jnp.float32)
+            block = block + jnp.dot(pick, lower, preferred_element_type=jnp.float32)
+            for h in range(2):
+                part = block[:, h * wide : (h + 1) * wide]
+                zhold[m, h, :, :, zs * 2 + core] = part[:half].reshape(2, 2, cap, wide)
+                zcout[m, zs, h] = part[half:].reshape(2, 2, cap, wide)
+            pair_core(m, zs).start()
+
+    def pair_product(m, h, away):
+        xx = 1 - x if away and h == 1 else x
+        yy = 1 - y if away and h == 0 else y
+        stack = []
+        for side, ref in enumerate((zhold.at[m, h, xx, yy], zxin.at[m, h, yy if h == 0 else xx])):
+            for s in range(4):
+                got = zmgot[(1 + h) * 2 * side + s % 2, pl.ds(m * 4 + s // 2 * 2 + xx, 1)]
+                label = jnp.where(
+                    yy == 1,
+                    jnp.concatenate([got[:, cap:]] * 2, axis=1),
+                    jnp.concatenate([got[:, :cap]] * 2, axis=1),
+                )
+                n = side * 4 + s
+                zhit[:, n * LANES : (n + 1) * LANES] = (cluster == label).astype(jnp.bfloat16)
+                stack.extend(pieces(ref[s], rep))
+        return jnp.dot(
+            zhit[...], jnp.concatenate(stack, axis=0), preferred_element_type=jnp.float32
+        )
+
+    def pair_send(m):
+        if m == 0:
+            drain(zmgot.at[pl.ds(0, 5)], zmrecv)
+        for h in range(2):
+            zsout[m, h] = pair_product(m, h, True)
+            pair_sums(m, h).start()
+
+    def pair_arrange(m):
+        for h in range(2):
+            columns = slice(h * wide, (h + 1) * wide)
+            own = zzout if m == 0 else zzown
+            own[:, columns] = pair_product(m, h, False)
+        drain(zsin.at[m], xsrecv.at[m])
+        for h in range(2):
+            columns = slice(h * wide, (h + 1) * wide)
+            own = zzout if m == 0 else zzown
+            own[:, columns] += zsin[m, h]
+        if m == 0:
+            pair_line().start()
+
+    def pair_conclude():
+        pair_line().wait_recv()
+        for h in range(2):
+            columns = slice(h * wide, (h + 1) * wide)
+            value = zzown[:, columns] + zzin[:, columns]
+            if alone:
+                lengths[...] += value * value
+                value = value * inverse[...]
+            main_ref[:, columns] = value
+
     load_label().start()
-    load(0).start()
+    load(shift).start()
     barrier = pltpu.get_barrier_semaphore()
     for d in range(1, inner):
         peer = plane * inner + across(d)
@@ -356,57 +494,50 @@
         peer = lax.rem(plane + d, outer) * inner + seat
         pl.semaphore_signal(barrier, inc=1, device_id={"dev": peer}, device_id_type=MESH)
 
-    target = route()
-    pick = picks(0, target)
-    split(0)
-    for c in range(1, chunks):
-        load(c).start()
+    load_label().wait()
+    target = route(label_ref[...])
+    pick = picks(target_plane(0), target)
+    split(shift)
+    for c in range(width // chunk):
+        if c != shift:
+            load(c).start()
     gather(0, pick, 0, half)
     pl.semaphore_wait(barrier, inner + outer - 2)
     for h in range(2):
         first_copy(0, h, 0).start()
+    if paired:
+        pair_label().start()
+        pair_rows().start()
     gather(0, pick, half, 2 * half)
     core_copy(0).start()
-    ready = 1
-
-    def prepare(pick):
-        nonlocal ready
-        t = ready
-        if t < steps:
-            if t < chunks:
-                split(t)
-            if t % chunks == 0:
-                pick = picks(t // chunks, target)
-            gather(t, pick)
-            core_copy(t).start()
-            ready += 1
-        return pick
-
-    split(1)
-    gather(1, pick, 0, half)
-    for h in range(2):
-        first_copy(1, h, 0).start()
-    gather(1, pick, half, 2 * half)
-    core_copy(1).start()
-    ready = 2
-    core_arrival(0).wait_recv()
-    for h in range(2):
-        first_copy(0, h, 1).start()
-    for h in range(2):
-        direct_copy(0, h).start()
-    pick = prepare(pick)
-    core_arrival(1).wait_recv()
-    for h in range(2):
-        first_copy(1, h, 1).start()
-    while ready < chunks:
-        pick = prepare(pick)
-    tell()
-    for j in range(outer):
-        tell_slots(j, picks(j, target))
-    for d in range(1, inner):
-        meta_copy(d).start()
-
-    waiting = []
+
+    def prepare(t):
+        nonlocal pick
+        if t < chunks:
+            split(t + shift)
+        if t % chunks == 0:
+            pick = picks(target_plane(t // chunks), target)
+        gather(t, pick)
+        core_copy(t).start()
+
+    def push(t):
+        core_arrival(t).wait_recv()
+        for h in range(2):
+            first_copy(t, h, parts_of(t) - 1).start()
+
+    def pair_push(m):
+        drain(zcout.at[m], xcrecv.at[m])
+        for h in range(2):
+            pair_first(m, h).start()
+
+    def direct(t):
+        for h in range(2):
+            direct_copy(t, h).start()
+
+    def head(t):
+        drain(xin.at[t], frecv.at[t])
+        for h in range(2):
+            passed_copy(t, h).start()
 
     def arrange(t):
         j, c = t // chunks, t % chunks
@@ -416,36 +547,114 @@
             if c == 0:
                 collect()
             conclude(c)
-        else:
-            reduce(j, c)
-
-            @pl.when(jnp.logical_not(fed(j)))
-            def _():
-                line_copy(j, c).start()
-
+            return
+        reduce(j, c)
+
+        @pl.when(jnp.logical_not(fed(j)))
+        def _():
+            line_copy(j, c).start()
+
+    split(1 + shift)
+    gather(1, pick, 0, half)
+    for h in range(2):
+        first_copy(1, h, 0).start()
+    gather(1, pick, half, 2 * half)
+    core_copy(1).start()
+    push(0)
+    direct(0)
+    prepare(2)
+    push(1)
+    if paired:
+        split(0)
+    tell()
+    for j in range(outer - 1):
+        tell_slots(j, picks(target_plane(j), target))
+    head(0)
+    tell_slots(last, picks(target_plane(last), target))
+    for d in range(1, inner):
+        meta_copy(d).start()
+    push(2)
+    direct(1)
+    prepare(3)
+
+    if paired:
+        head(1)
+        push(3)
+        direct(2)
+        pair_label().wait_recv()
+        pair_target = route(zlabel[...])
+        pair_tell(pair_target)
+        prepare(4)
+        arrange(0)
+
+        head(2)
+        push(4)
+        direct(3)
+        prepare(5)
+        arrange(1)
+
+        head(3)
+        push(5)
+        direct(4)
+        arrange(2)
+        pair_gather(0, pair_target)
+
+        head(4)
+        pair_push(0)
+        direct(5)
+        prepare(6)
+        arrange(3)
+
+        head(5)
+        forward(0, 0)
+        pair_gather(1, pair_target)
+        arrange(4)
+        forward(0, 1)
+        pair_push(1)
+
+        drain(zxin.at[0], xfrecv.at[0])
+        pair_send(0)
+        push(6)
+        prepare(7)
+        forward(2, 0)
+        arrange(5)
+        forward(1, 0)
+        forward(2, 1)
+
+        drain(zxin.at[1], xfrecv.at[1])
+        pair_send(1)
+        push(7)
+        direct(6)
+        forward(1, 1)
+        pair_arrange(0)
+
+        head(6)
+        direct(7)
+        pair_arrange(1)
+
+        head(7)
+        arrange(6)
+        arrange(7)
+        pair_conclude()
+    else:
+        waiting = []
+        for t in range(1, steps + 1):
+            if t < steps:
+                head(t)
+            if t + 2 < steps:
+                push(t + 2)
+            if t + 1 < steps:
+                direct(t + 1)
+            if t + 3 < steps:
+                prepare(t + 3)
+            arrange(t - 1)
+            j, c = (t - 1) // chunks, (t - 1) % chunks
             if j == last - 1:
                 forward(j, c)
-            else:
+            elif j < last:
                 waiting.append((j, c))
-        while waiting and (len(waiting) > 2 or t >= last * chunks - 1):
-            forward(*waiting.pop(0))
-
-    for t in range(steps):
-        drain(xin.at[t], frecv.at[t])
-        for h in range(2):
-            passed_copy(t, h).start()
-        if t + 2 < steps:
-            core_arrival(t + 2).wait_recv()
-            for h in range(2):
-                first_copy(t + 2, h, 0).start()
-        if t + 1 < steps:
-            for h in range(2):
-                direct_copy(t + 1, h).start()
-        pick = prepare(pick)
-        if t > 0:
-            arrange(t - 1)
-
-    arrange(steps - 1)
+            while waiting and (len(waiting) > 2 or t >= last * chunks):
+                forward(*waiting.pop(0))
     if alone:
         denom = jnp.maximum(aux_all[0:1, :], 1.0)
         squares = aux_all[1:2, :] + aux_all[2:3, :] + aux_all[3:4, :]
@@ -462,6 +671,14 @@
     if last:
         drain(zout, zsend)
         drain(zaux, asend)
+    if paired:
+        pair_label().wait_send()
+        pair_rows().wait_send()
+        drain(zmgot.at[pl.ds(0, 5)], zmsend)
+        drain(zcout, xcsend)
+        drain(zxin, xfsend)
+        drain(zsout, xssend)
+        pair_line().wait_send()
 
 
 def body(points, assignment):
@@ -471,7 +688,8 @@
     cap = 2 * rows // owners
     outer = owners // INNER
     chunk = 2 * LANES
-    chunks = width // chunk
+    paired = outer == 4 and 2 * cap == LANES and width == 3 * chunk
+    chunks = width // chunk - (1 if paired else 0)
     wide = chunk // 2
     steps = outer * chunks
     ring = min(steps, 4)
@@ -480,10 +698,31 @@
     dma = pltpu.SemaphoreType.DMA
     hops = max(outer - 1, 1)
     side = (1, CL_OWN) if alone else (8, CL_OWN)
+    extra = [
+        pltpu.VMEM((1, rows), jnp.int32),
+        pltpu.VMEM((rows, chunk), f32),
+        pltpu.VMEM((rows, chunk), b16),
+        pltpu.VMEM((rows, chunk), b16),
+        pltpu.VMEM((8, rows), b16),
+        pltpu.VMEM((2, 2, 2, 2, 4, cap, wide), f32),
+        pltpu.VMEM((2, 2, 2, 2, 2, cap, wide), f32),
+        pltpu.VMEM((2, 2, 2, 4, cap, wide), f32),
+        pltpu.VMEM((2, 2, CL_OWN, wide), f32),
+        pltpu.VMEM((2, 2, CL_OWN, wide), f32),
+        pltpu.VMEM((CL_OWN, chunk), f32),
+        pltpu.VMEM((CL_OWN, chunk), f32),
+        pltpu.VMEM((CL_OWN, chunk), f32),
+        pltpu.VMEM((2, 8, LANES), f32),
+        pltpu.VMEM((6, 8, LANES), f32),
+        pltpu.VMEM((CL_OWN, INNER * LANES), b16),
+        dma(()), dma(()), dma(()), dma(()),
+        dma(()), dma((2,)), dma(()), dma((2,)),
+        dma(()), dma((2,)), dma(()), dma(()), dma(()), dma(()),
+    ]
     vmem = pl.BlockSpec(memory_space=pltpu.VMEM)
     hbm = pl.BlockSpec(memory_space=pltpu.HBM)
     main, side = pl.pallas_call(
-        functools.partial(kernel, outer, cap, chunk, alone),
+        functools.partial(kernel, outer, cap, chunk, alone, paired),
         out_shape=(
             jax.ShapeDtypeStruct((CL_OWN, width), f32),
             jax.ShapeDtypeStruct(side, f32),
@@ -492,7 +731,7 @@
         out_specs=[vmem, vmem],
         scratch_shapes=[
             pltpu.VMEM((1, rows), jnp.int32),
-            pltpu.VMEM((chunks, rows, chunk), f32),
+            pltpu.VMEM((width // chunk, rows, chunk), f32),
             pltpu.VMEM((rows, width), b16),
             pltpu.VMEM((rows, width), b16),
             pltpu.VMEM((rows, LANES), f32),
@@ -512,14 +751,14 @@
             pltpu.VMEM((8, CL_OWN), f32),
             pltpu.VMEM((CL_OWN, LANES), f32),
             pltpu.VMEM((CL_OWN, LANES), f32),
-            dma((chunks + 1,)),
+            dma((width // chunk + 1,)),
             dma(()), dma(()),
             dma((ring,)), dma((steps,)),
             dma(()), dma((steps,)),
             dma(()), dma((steps + 1,)),
             dma(()), dma((outer + 1, chunks)),
             dma(()), dma(()),
-        ],
+        ] + (extra if paired else []),
         compiler_params=pltpu.CompilerParams(
             collective_id=0, has_side_effects=True, vmem_limit_bytes=LIMIT
         ),

time: 78.5 us -> 76.3 us (0.972)
  Pallas kernels: 76.2 us -> 74 us
    pallas_call x1, Pallas kernels: 76.2 us -> 74 us  [body(): pl.pallas_call(functools.partial(kernel, outer, cap, chunk, alone, paired...]
where the time goes in v3:
time: 76.3 us; the launch traced here: 76.1 us
  Pallas kernels  74 us (97%)
  local copies, waits for them, and re-layouts  1.44 us (2%)
    pallas_call x1, Pallas kernels, body(): pl.pallas_call(functools.partial(kernel, outer, cap, chunk, alone, paired...  74 us

profile of v3, /device:TPU:0, one launch (start us, length us, event | category | flops | bytes accessed | tf_op | source)
XLA Modules:
  0.0 76.1 jit_solution(6465407553562414218)
XLA Ops:
  0.6 74.0 %shard_map.41 = (f32[256,768]{1,0:T(8,128)S(1)}, f32[1,256]{1,0:T(1,128)S(1)}) custom-call(f32[1024,768]{1,0:T(8,128)} %points_ref.1, s32[1,1024]{1,0:T(1,128)} %bitcast.3), custom_call_target="tpu_custom_call" | custom-call | tf_op jit(solution)/shard_map/pallas_call | solution.py:724
  74.7 0.9 %copy.6 = f32[256,768]{1,0:T(8,128)} copy(f32[256,768]{1,0:T(8,128)S(1)} %get-tuple-element.8) | data formatting | bytes 1572864
  75.6 0.6 copy.7

commit v4 on v3

--- a/solution.py
+++ b/solution.py
@@ -602,11 +602,11 @@
         head(4)
         pair_push(0)
         direct(5)
+        forward(0, 0)
         prepare(6)
         arrange(3)
 
         head(5)
-        forward(0, 0)
         pair_gather(1, pair_target)
         arrange(4)
         forward(0, 1)
@@ -617,15 +617,15 @@
         push(6)
         prepare(7)
         forward(2, 0)
+        forward(1, 0)
         arrange(5)
-        forward(1, 0)
         forward(2, 1)
+        forward(1, 1)
 
         drain(zxin.at[1], xfrecv.at[1])
         pair_send(1)
         push(7)
         direct(6)
-        forward(1, 1)
         pair_arrange(0)
 
         head(6)

time: 76.3 us -> 75 us (0.983)
  Pallas kernels: 74 us -> 72.8 us
    pallas_call x1, Pallas kernels: 74 us -> 72.8 us  [body(): pl.pallas_call(functools.partial(kernel, outer, cap, chunk, alone, paired...]
where the time goes in v4:
time: 75 us; the launch traced here: 74.8 us
  Pallas kernels  72.8 us (97%)
  local copies, waits for them, and re-layouts  1.44 us (2%)
    pallas_call x1, Pallas kernels, body(): pl.pallas_call(functools.partial(kernel, outer, cap, chunk, alone, paired...  72.8 us

profile of v4, /device:TPU:0, one launch (start us, length us, event | category | flops | bytes accessed | tf_op | source)
XLA Modules:
  0.0 74.8 jit_solution(1328618419718713377)
XLA Ops:
  0.6 72.8 %shard_map.41 = (f32[256,768]{1,0:T(8,128)S(1)}, f32[1,256]{1,0:T(1,128)S(1)}) custom-call(f32[1024,768]{1,0:T(8,128)} %points_ref.1, s32[1,1024]{1,0:T(1,128)} %bitcast.3), custom_call_target="tpu_custom_call" | custom-call | tf_op jit(solution)/shard_map/pallas_call | solution.py:724
  73.4 0.9 %copy.6 = f32[256,768]{1,0:T(8,128)} copy(f32[256,768]{1,0:T(8,128)S(1)} %get-tuple-element.8) | data formatting | bytes 1572864
  74.3 0.6 copy.7
